TPU v7x, 32 devices: a whole 2x2x4 slice. The times are simulated.
32 devices in a mesh: row: 4 (over x, core), col: 8 (over z, y).
Axes of the slice: x: 2, y: 2, z: 4, core: 2. Of those that a mesh axis runs over, the one named last changes fastest.
Arguments:
- points: float32 [16, 8192], P(None, ('row', 'col')), may hold values from -6 to 6
- lengthscale: float32 [16], replicated, may hold values from 2 to 8
- signal: float32 [1], replicated, may hold values from 0.5 to 2
- noise: float32 [1], replicated, may hold values from 0.05 to 0.5
- targets: float32 [8192], P(('row', 'col')), may hold values from -12 to 12
- probe_bits: int32 [31, 8192], P(None, ('row', 'col')), may hold values from 0 to 1
Outputs:
- solution: float32 [32, 8192], P(None, ('row', 'col'))
- residual: float32 [32, 8192], P(None, ('row', 'col'))
All inputs are finite; a program needn't handle non-finite values.
Results may differ from a plain program's by a relative error of at most 0.0013.
Values sent between devices are 32-bit elements; how exact they have to be, the bound alone decides.
No kernel may reach another device: no remote copies, remote signals or barrier semaphores. Data moves between devices by JAX's collectives and lax.ppermute only.
A program may use at most 128 MiB of HBM per device.

v0:
```python
import jax
import jax.numpy as jnp
from jax import lax
from jax.sharding import PartitionSpec as P

ITERS = 3
ROOT_FIVE = 5.0**0.5


def matern_tile(row_scaled, col_scaled, signal_value):
    row_sq = jnp.sum(row_scaled * row_scaled, axis=0)
    col_sq = jnp.sum(col_scaled * col_scaled, axis=0)
    cross_term = lax.dot_general(
        row_scaled,
        col_scaled,
        (((0,), (0,)), ((), ())),
        precision=lax.Precision.HIGHEST,
        preferred_element_type=jnp.float32,
    )
    dist_sq = jnp.maximum(row_sq[:, None] + col_sq[None, :] - 2.0 * cross_term, 0.0)
    radius = jnp.sqrt(dist_sq)
    return (
        signal_value
        * (1.0 + ROOT_FIVE * radius + 5.0 / 3.0 * dist_sq)
        * jnp.exp(-ROOT_FIVE * radius)
    )


def row_blocks(row_scaled):
    row_total = row_scaled.shape[1]
    block_rows = min(1024, row_total)
    block_count = row_total // block_rows
    return row_scaled.reshape(row_scaled.shape[0], block_count, block_rows).transpose(1, 0, 2)


def apply_tile(row_scaled, col_scaled, signal_value, vectors):
    row_total = row_scaled.shape[1]
    stacked = row_blocks(row_scaled)

    def one_block(row_block):
        kernel_tile = matern_tile(row_block, col_scaled, signal_value)
        return lax.dot_general(
            vectors,
            kernel_tile,
            (((1,), (1,)), ((), ())),
            precision=lax.Precision.HIGHEST,
            preferred_element_type=jnp.float32,
        )

    pieces = lax.map(one_block, stacked)
    return pieces.transpose(1, 0, 2).reshape(vectors.shape[0], row_total)


def squares(residual):
    return lax.psum(jnp.sum(residual * residual, axis=1), ("row", "col"))


def body(points, lengthscale, signal, noise, targets, probe_bits):
    scaled = points / lengthscale[:, None]
    signs = 2.0 * probe_bits.astype(jnp.float32) - 1.0
    right_side = jnp.concatenate([targets[None, :], signs], axis=0)
    signal_value = signal[0]
    noise_value = noise[0]
    every_point = lax.all_gather(scaled, ("row", "col"), axis=1, tiled=True)
    solution = jnp.zeros_like(right_side)
    residual = right_side
    direction = right_side
    norm_now = squares(residual)
    for step in range(ITERS):
        summed = apply_tile(
            scaled,
            every_point,
            signal_value,
            lax.all_gather(direction, ("row", "col"), axis=1, tiled=True),
        )
        image = summed + noise_value * direction
        curved = lax.psum(jnp.sum(direction * image, axis=1), ("row", "col"))
        alpha = norm_now / curved
        solution = solution + alpha[:, None] * direction
        residual = residual - alpha[:, None] * image
        if step + 1 < ITERS:
            norm_next = squares(residual)
            direction = residual + (norm_next / norm_now)[:, None] * direction
            norm_now = norm_next
    return (solution, residual)


def solution(mesh):
    return jax.shard_map(
        body,
        mesh=mesh,
        in_specs=(
            P(None, ("row", "col")),
            P(),
            P(),
            P(),
            P(("row", "col")),
            P(None, ("row", "col")),
        ),
        out_specs=(P(None, ("row", "col")), P(None, ("row", "col"))),
        check_vma=False,
    )
```

profile of v0, /device:TPU:0, one launch (start us, length us, event | category | flops | bytes accessed | tf_op | source)
XLA Modules:
  0.0 442.8 jit_solution(3945853298160864915)
XLA Ops:
  7.2 0.0 all-gather.4.cloned.1.call-start
  7.2 0.8 multiply_add_fusion.3
  8.0 1.3 pad_maximum_fusion
  9.3 0.0 all-gather.4.cloned.1.call-update
  9.3 0.0 all-gather.6.cloned.1.call-start
  10.6 0.8 multiply_reduce_fusion.7
  11.5 73.2 %all_gather.13 = f32[16,8192]{1,0:T(8,128)S(1)} all-gather(f32[16,256]{1,0:T(8,128)S(1)} %get-tuple-element.51), channel_id=1, replica_groups=mesh['row'=4,'col'=8] {'row','col'}, dimensions={1}, use_global_device_ids=true | all-gather | bytes 540672 | tf_op jit(solution)/shard_map/all_gather | solution.py:64
  84.6 0.1 multiply_reduce_fusion
  84.7 0.0 copy-start.2
  84.7 14.0 %exponential_multiply_fusion = f32[256,8192]{1,0:T(8,128)} fusion(f32[16,256]{1,0:T(8,128)S(1)} %get-tuple-element.51, f32[16,8192]{1,0:T(8,128)S(1)} %all_gather.13, f32[8192]{0:T(1024)S(1)} %multiply_reduce_fusion, f32[256]{0:T(256)S(1)} %get-tuple-element.50, f32[]{:T(128)} %bitcast.11), kind=kOutput, calls=%fused_computation.3 | convolution fusion | flops 425721856 | bytes 8963076 | tf_op jit(solution)/shard_map/while/body/eval_jaxpr/dot_general | solution.py:13
  98.7 0.0 copy-start.3
  98.7 0.0 all-gather.4.cloned.1.call-done
  98.7 0.0 copy-done.2
  98.8 11.2 %multiply_reduce_fusion.5 = (f32[32]{0:T(128)S(1)}, f32[32]{0:T(128)S(1)}, f32[32,256]{1,0:T(8,128)S(1)}) fusion(f32[32,256]{1,0:T(8,128)S(1)} %copy-done.2, f32[]{:T(128)} %bitcast.12, f32[32,8192]{1,0:T(8,128)} %all-gather.4.cloned.1.call-done, f32[256,8192]{1,0:T(8,128)} %exponential_multiply_fusion), kind=kOutput, calls=%fused_computation.19 | convolution fusion | flops 805355456 | bytes 9502980 | tf_op jit(solution)/shard_map/while/body/eval_jaxpr/dot_general | solution.py:42
  109.9 37.1 %all-reduce = (f32[32]{0:T(128)S(1)}, f32[32]{0:T(128)S(1)}) all-reduce(f32[32]{0:T(128)S(1)} %get-tuple-element.39, f32[32]{0:T(128)S(1)} %get-tuple-element.38), channel_id=1, replica_groups=mesh['row'=4,'col'=8] {'row','col'}, use_global_device_ids=true, to_apply=%region_1.0 | all-reduce | flops 64 | bytes 512 | tf_op jit(solution)/shard_map/psum | solution.py:55
  147.0 0.0 copy-done.3
  147.0 0.2 multiply_reduce_fusion.4
  147.2 41.5 %psum.44 = f32[32]{0:T(128)S(1)} all-reduce(f32[32]{0:T(128)S(1)} %multiply_reduce_fusion.4), channel_id=1, replica_groups=mesh['row'=4,'col'=8] {'row','col'}, use_global_device_ids=true, to_apply=%region_7.8 | all-reduce | flops 32 | bytes 256 | tf_op jit(solution)/shard_map/psum | solution.py:55
  188.7 0.7 multiply_add_fusion.2
  189.4 0.0 copy-start
  189.4 0.0 all-gather.6.cloned.1.call-update
  189.5 0.0 all-gather.8.cloned.1.call-start
  189.5 51.3 %all-gather.6.cloned.1.call-done = f32[32,8192]{1,0:T(8,128)} async-done(((f32[32,256]{1,0:T(8,128)}), f32[32,8192]{1,0:T(8,128)}) %all-gather.6.cloned.1.call-update) | async-done | bytes 1048592 | tf_op jit(solution)/shard_map/all_gather | solution.py:74
  240.8 11.1 %multiply_reduce_fusion.3 = (f32[32]{0:T(128)S(1)}, f32[32,256]{1,0:T(8,128)S(1)}) fusion(f32[32,256]{1,0:T(8,128)} %multiply_add_fusion.2, f32[]{:T(128)} %bitcast.14, f32[32,8192]{1,0:T(8,128)} %all-gather.6.cloned.1.call-done, f32[256,8192]{1,0:T(8,128)} %exponential_multiply_fusion), kind=kOutput, calls=%fused_computation.15 | convolution fusion | flops 805339136 | bytes 9502852 | tf_op jit(solution)/shard_map/while/body/eval_jaxpr/dot_general | solution.py:42
  251.9 40.3 %psum.45 = f32[32]{0:T(128)S(1)} all-reduce(f32[32]{0:T(128)S(1)} %get-tuple-element.61), channel_id=1, replica_groups=mesh['row'=4,'col'=8] {'row','col'}, use_global_device_ids=true, to_apply=%region_9.10 | all-reduce | flops 32 | bytes 256 | tf_op jit(solution)/shard_map/psum | solution.py:77
  292.1 0.2 multiply_reduce_fusion.2
  292.3 39.2 %psum.46 = f32[32]{0:T(128)S(1)} all-reduce(f32[32]{0:T(128)S(1)} %get-tuple-element.48), channel_id=1, replica_groups=mesh['row'=4,'col'=8] {'row','col'}, use_global_device_ids=true, to_apply=%region_11.12 | all-reduce | flops 32 | bytes 256 | tf_op jit(solution)/shard_map/psum | solution.py:55
  331.5 0.0 copy-done
  331.5 0.7 multiply_add_fusion.1
  332.2 0.0 copy-start.1
  332.2 0.0 all-gather.8.cloned.1.call-update
  332.3 52.0 %all-gather.8.cloned.1.call-done = f32[32,8192]{1,0:T(8,128)} async-done(((f32[32,256]{1,0:T(8,128)}), f32[32,8192]{1,0:T(8,128)}) %all-gather.8.cloned.1.call-update) | async-done | bytes 1048592 | tf_op jit(solution)/shard_map/all_gather | solution.py:74
  384.2 11.1 %multiply_reduce_fusion.1 = (f32[32]{0:T(128)S(1)}, f32[32,256]{1,0:T(8,128)S(1)}) fusion(f32[32,256]{1,0:T(8,128)} %multiply_add_fusion.1, f32[]{:T(128)} %bitcast.13, f32[32,8192]{1,0:T(8,128)} %all-gather.8.cloned.1.call-done, f32[256,8192]{1,0:T(8,128)} %exponential_multiply_fusion), kind=kOutput, calls=%fused_computation.11 | convolution fusion | flops 805339136 | bytes 9502852 | tf_op jit(solution)/shard_map/while/body/eval_jaxpr/dot_general | solution.py:42
  395.3 40.3 %psum.47 = f32[32]{0:T(128)S(1)} all-reduce(f32[32]{0:T(128)S(1)} %get-tuple-element.63), channel_id=1, replica_groups=mesh['row'=4,'col'=8] {'row','col'}, use_global_device_ids=true, to_apply=%region_13.14 | all-reduce | flops 32 | bytes 256 | tf_op jit(solution)/shard_map/psum | solution.py:77
  435.5 0.0 copy-done.1
  435.5 0.7 multiply_subtract_fusion
  (5 shorter events, 0.0 us)
Async XLA Ops:
  7.2 91.6 %all-gather.4.cloned.1.call-start = ((), (), s32[]{:S(2)}) async-start(), calls=%async_computation | async-start | bytes 1081344 | tf_op jit(solution)/shard_map/all_gather | solution.py:74
  9.3 231.5 %all-gather.6.cloned.1.call-start = ((), (), s32[]{:S(2)}) async-start(), calls=%async_computation.1 | async-start | bytes 1081344 | tf_op jit(solution)/shard_map/all_gather | solution.py:74
  84.7 14.0 %copy-start.2 = (f32[32,256]{1,0:T(8,128)S(1)}, f32[32,256]{1,0:T(8,128)}, u32[]{:S(2)}) copy-start(f32[32,256]{1,0:T(8,128)} %pad_maximum_fusion) | copy-start | bytes 98308
  98.7 48.3 %copy-start.3 = (f32[256]{0:T(256)S(1)}, f32[256]{0:T(256)}, u32[]{:S(2)}) copy-start(f32[256]{0:T(256)} %param.10) | copy-start | bytes 3076
  189.4 142.1 %copy-start = (f32[32,256]{1,0:T(8,128)S(1)}, f32[32,256]{1,0:T(8,128)}, u32[]{:S(2)}) copy-start(f32[32,256]{1,0:T(8,128)} %multiply_add_fusion.2) | copy-start | bytes 98308
  189.5 194.7 %all-gather.8.cloned.1.call-start = ((), (), s32[]{:S(2)}) async-start(), calls=%async_computation.2 | async-start | bytes 1081344 | tf_op jit(solution)/shard_map/all_gather | solution.py:74
  332.2 103.3 %copy-start.1 = (f32[32,256]{1,0:T(8,128)S(1)}, f32[32,256]{1,0:T(8,128)}, u32[]{:S(2)}) copy-start(f32[32,256]{1,0:T(8,128)} %multiply_add_fusion.1) | copy-start | bytes 98308
Sparse Core Ops, SparseCore 0:
  11.4 54.6 all-gather.3
  189.6 51.1 all-gather.5
  332.4 51.7 all-gather.7
where the time goes:
time: 444 us; the launch traced here: 443 us
  blocking collectives  272 us (61%)
  waiting for transfers between devices  103 us (23%)
  matrix products  47.3 us (11%)
  between operations  15.1 us (3%)
  other arithmetic  5.46 us (1%)
    psum x3, blocking collectives, squares(): return lax.psum(jnp.sum(residual * residual, axis=1), ('row', 'col'))  118 us
    all_gather x3, waiting for transfers between devices, body(): lax.all_gather(direction, ('row', 'col'), axis=1, tiled=True)  103 us
    psum x2, blocking collectives, body(): curved = lax.psum(jnp.sum(direction * image, axis=1), ('row', 'col'))  80.5 us
    all_gather x1, blocking collectives, body(): every_point = lax.all_gather(scaled, ('row', 'col'), axis=1, tiled=True)  73.2 us
    dot_general x3, matrix products, one_block(): lax.dot_general(vectors, kernel_tile, (((1,), (1,)), ((), ())), precision...  33.3 us
    dot_general x1, matrix products, matern_tile(): lax.dot_general(row_scaled, col_scaled, (((0,), (0,)), ((), ())), precisi...  14 us
  transfers between devices with their start and end apart: 3, of which 2 were waited for; matrix products, arithmetic and copies ran while one was open for 3% of the time, Pallas kernels for 0%

commit v1 on v0

--- a/solution.py
+++ b/solution.py
@@ -5,6 +5,12 @@
 
 ITERS = 3
 ROOT_FIVE = 5.0**0.5
+
+
+def pass_the_trees(frame):
+    tile_out = jnp.stack([frame for _ in range(jax.lax.axis_size(("row", "col")))])
+    ready = jax.lax.all_to_all(tile_out, ("row", "col"), 0, 0)
+    return jnp.concatenate(ready, axis=1)
 
 
 def matern_tile(row_scaled, col_scaled, signal_value):
@@ -67,12 +73,7 @@
     direction = right_side
     norm_now = squares(residual)
     for step in range(ITERS):
-        summed = apply_tile(
-            scaled,
-            every_point,
-            signal_value,
-            lax.all_gather(direction, ("row", "col"), axis=1, tiled=True),
-        )
+        summed = apply_tile(scaled, every_point, signal_value, pass_the_trees(direction))
         image = summed + noise_value * direction
         curved = lax.psum(jnp.sum(direction * image, axis=1), ("row", "col"))
         alpha = norm_now / curved

time: 444 us -> 400 us (0.901)
  waiting for transfers between devices: 103 us -> 0.01 us
  blocking collectives: 272 us -> 341 us
  between operations: 15.1 us -> 2 us
  starting transfers between devices: 0.12 us -> 7.33 us
    all_gather x3 -> x0, waiting for transfers between devices: 103 us -> none  [body(): lax.all_gather(direction, ('row', 'col'), axis=1, tiled=True)]
    all_to_all x0 -> x2, blocking collectives: none -> 63 us  [pass_the_trees(): ready = jax.lax.all_to_all(tile_out, ('row', 'col'), 0, 0)]
    all_gather x1, blocking collectives: 73.2 us -> 82.9 us  [body(): every_point = lax.all_gather(scaled, ('row', 'col'), axis=1, tiled=True)]
    all_to_all x0 -> x1, starting transfers between devices: none -> 7.33 us  [pass_the_trees(): ready = jax.lax.all_to_all(tile_out, ('row', 'col'), 0, 0)]
    psum x2, blocking collectives: 80.5 us -> 75.9 us  [body(): curved = lax.psum(jnp.sum(direction * image, axis=1), ('row', 'col'))]
  transfers between devices with their start and end apart: 3 -> 1, of which waited for: 2 -> 0; matrix products, arithmetic and copies ran while one was open for 3% -> 4% of each run, Pallas kernels for 0% -> 0%
where the time goes in v1:
time: 400 us; the launch traced here: 399 us
  blocking collectives  341 us (85%)
  matrix products  43.5 us (11%)
  starting transfers between devices  7.33 us (2%)
    psum x3, blocking collectives, squares(): return lax.psum(jnp.sum(residual * residual, axis=1), ('row', 'col'))  119 us
    all_gather x1, blocking collectives, body(): every_point = lax.all_gather(scaled, ('row', 'col'), axis=1, tiled=True)  82.9 us
    psum x2, blocking collectives, body(): curved = lax.psum(jnp.sum(direction * image, axis=1), ('row', 'col'))  75.9 us
    all_to_all x2, blocking collectives, pass_the_trees(): ready = jax.lax.all_to_all(tile_out, ('row', 'col'), 0, 0)  63 us
    dot_general x3, matrix products, one_block(): lax.dot_general(vectors, kernel_tile, (((1,), (1,)), ((), ())), precision...  29.5 us
    dot_general x1, matrix products, matern_tile(): lax.dot_general(row_scaled, col_scaled, (((0,), (0,)), ((), ())), precisi...  14 us
  transfers between devices with their start and end apart: 1, of which 0 were waited for; matrix products, arithmetic and copies ran while one was open for 4% of the time, Pallas kernels for 0%

profile of v1, /device:TPU:0, one launch (start us, length us, event | category | flops | bytes accessed | tf_op | source)
XLA Modules:
  0.0 399.0 jit_solution(8145861089506825722)
XLA Ops:
  0.6 0.8 multiply_add_fusion.3
  1.4 0.7 pad_maximum_fusion
  2.1 1.2 stack.6
  3.3 7.3 %all-to-all-start = ((f32[32,32,256]{2,1,0:T(8,128)}), f32[32,32,256]{2,1,0:T(8,128)S(1)}, u32[]{:S(2)}, u32[]{:S(2)}) async-start(f32[32,32,256]{2,1,0:T(8,128)} %stack.6), calls=%async_computation | async-start | bytes 2097152 | tf_op jit(solution)/shard_map/all_to_all | solution.py:12
  11.9 0.8 multiply_reduce_fusion.7
  12.7 82.9 %all_gather.3 = f32[16,8192]{1,0:T(8,128)S(1)} all-gather(f32[16,256]{1,0:T(8,128)S(1)} %get-tuple-element.51), channel_id=1, replica_groups=mesh['row'=4,'col'=8] {'row','col'}, dimensions={1}, use_global_device_ids=true | all-gather | bytes 540672 | tf_op jit(solution)/shard_map/all_gather | solution.py:70
  95.6 0.1 multiply_reduce_fusion
  95.7 14.0 %exponential_multiply_fusion = f32[256,8192]{1,0:T(8,128)} fusion(f32[16,256]{1,0:T(8,128)S(1)} %get-tuple-element.51, f32[16,8192]{1,0:T(8,128)S(1)} %all_gather.3, f32[8192]{0:T(1024)S(1)} %multiply_reduce_fusion, f32[256]{0:T(256)S(1)} %get-tuple-element.50, f32[]{:T(128)} %bitcast.20), kind=kOutput, calls=%fused_computation.3 | convolution fusion | flops 425721856 | bytes 8963076 | tf_op jit(solution)/shard_map/while/body/eval_jaxpr/dot_general | solution.py:19
  109.7 0.0 copy-start
  109.7 0.0 all-to-all-done
  109.7 0.1 copy.11
  109.8 9.8 %multiply_reduce_fusion.5 = (f32[32]{0:T(128)S(1)}, f32[32]{0:T(128)S(1)}, f32[32,256]{1,0:T(8,128)S(1)}) fusion(f32[32,256]{1,0:T(8,128)S(1)} %pad_maximum_fusion, f32[]{:T(128)} %bitcast.21, f32[32,8192]{1,0:T(8,128)S(1)} %bitcast.24, f32[256,8192]{1,0:T(8,128)} %exponential_multiply_fusion), kind=kOutput, calls=%fused_computation.19 | convolution fusion | flops 805355456 | bytes 9502980 | tf_op jit(solution)/shard_map/while/body/eval_jaxpr/dot_general | solution.py:48
  119.6 36.8 %all-reduce = (f32[32]{0:T(128)S(1)}, f32[32]{0:T(128)S(1)}) all-reduce(f32[32]{0:T(128)S(1)} %get-tuple-element.39, f32[32]{0:T(128)S(1)} %get-tuple-element.38), channel_id=1, replica_groups=mesh['row'=4,'col'=8] {'row','col'}, use_global_device_ids=true, to_apply=%region_1.0 | all-reduce | flops 64 | bytes 512 | tf_op jit(solution)/shard_map/psum | solution.py:61
  156.5 0.0 copy-done
  156.5 0.2 multiply_reduce_fusion.4
  156.6 41.9 %psum.44 = f32[32]{0:T(128)S(1)} all-reduce(f32[32]{0:T(128)S(1)} %multiply_reduce_fusion.4), channel_id=1, replica_groups=mesh['row'=4,'col'=8] {'row','col'}, use_global_device_ids=true, to_apply=%region_7.8 | all-reduce | flops 32 | bytes 256 | tf_op jit(solution)/shard_map/psum | solution.py:61
  198.5 0.1 multiply_add_fusion.2
  198.6 0.1 stack.7
  198.8 31.3 %all_to_all.15 = f32[32,32,256]{2,1,0:T(8,128)S(1)} all-to-all(f32[32,32,256]{2,1,0:T(8,128)S(1)} %stack.7), channel_id=1, replica_groups=mesh['row'=4,'col'=8] {'row','col'}, dimensions={0} | all-to-all | bytes 2097152 | tf_op jit(solution)/shard_map/all_to_all | solution.py:12
  230.1 0.1 copy.12
  230.1 9.8 %multiply_reduce_fusion.3 = (f32[32]{0:T(128)S(1)}, f32[32,256]{1,0:T(8,128)S(1)}) fusion(f32[32,256]{1,0:T(8,128)S(1)} %multiply_add_fusion.2, f32[]{:T(128)} %bitcast.23, f32[32,8192]{1,0:T(8,128)S(1)} %bitcast.26, f32[256,8192]{1,0:T(8,128)} %exponential_multiply_fusion), kind=kOutput, calls=%fused_computation.15 | convolution fusion | flops 805339136 | bytes 9502852 | tf_op jit(solution)/shard_map/while/body/eval_jaxpr/dot_general | solution.py:48
  240.0 38.0 %psum.45 = f32[32]{0:T(128)S(1)} all-reduce(f32[32]{0:T(128)S(1)} %get-tuple-element.61), channel_id=1, replica_groups=mesh['row'=4,'col'=8] {'row','col'}, use_global_device_ids=true, to_apply=%region_9.10 | all-reduce | flops 32 | bytes 256 | tf_op jit(solution)/shard_map/psum | solution.py:78
  277.9 0.2 multiply_reduce_fusion.2
  278.1 40.4 %psum.46 = f32[32]{0:T(128)S(1)} all-reduce(f32[32]{0:T(128)S(1)} %get-tuple-element.48), channel_id=1, replica_groups=mesh['row'=4,'col'=8] {'row','col'}, use_global_device_ids=true, to_apply=%region_11.12 | all-reduce | flops 32 | bytes 256 | tf_op jit(solution)/shard_map/psum | solution.py:61
  318.5 0.1 multiply_add_fusion.1
  318.6 0.1 stack.8
  318.8 31.7 %all_to_all.16 = f32[32,32,256]{2,1,0:T(8,128)S(1)} all-to-all(f32[32,32,256]{2,1,0:T(8,128)S(1)} %stack.8), channel_id=1, replica_groups=mesh['row'=4,'col'=8] {'row','col'}, dimensions={0} | all-to-all | bytes 2097152 | tf_op jit(solution)/shard_map/all_to_all | solution.py:12
  350.4 0.1 copy.13
  350.5 9.8 %multiply_reduce_fusion.1 = (f32[32]{0:T(128)S(1)}, f32[32,256]{1,0:T(8,128)S(1)}) fusion(f32[32,256]{1,0:T(8,128)S(1)} %multiply_add_fusion.1, f32[]{:T(128)} %bitcast.22, f32[32,8192]{1,0:T(8,128)S(1)} %bitcast.25, f32[256,8192]{1,0:T(8,128)} %exponential_multiply_fusion), kind=kOutput, calls=%fused_computation.11 | convolution fusion | flops 805339136 | bytes 9502852 | tf_op jit(solution)/shard_map/while/body/eval_jaxpr/dot_general | solution.py:48
  360.3 38.0 %psum.47 = f32[32]{0:T(128)S(1)} all-reduce(f32[32]{0:T(128)S(1)} %get-tuple-element.63), channel_id=1, replica_groups=mesh['row'=4,'col'=8] {'row','col'}, use_global_device_ids=true, to_apply=%region_13.14 | all-reduce | flops 32 | bytes 256 | tf_op jit(solution)/shard_map/psum | solution.py:78
  398.3 0.7 multiply_subtract_fusion
  (5 shorter events, 0.0 us)
Async XLA Ops:
  3.3 106.4 %all-to-all-start = ((f32[32,32,256]{2,1,0:T(8,128)}), f32[32,32,256]{2,1,0:T(8,128)S(1)}, u32[]{:S(2)}, u32[]{:S(2)}) async-start(f32[32,32,256]{2,1,0:T(8,128)} %stack.6), calls=%async_computation | async-start | bytes 2097152 | tf_op jit(solution)/shard_map/all_to_all | solution.py:12
  109.7 46.8 %copy-start = (f32[256]{0:T(256)S(1)}, f32[256]{0:T(256)}, u32[]{:S(2)}) copy-start(f32[256]{0:T(256)} %param.10) | copy-start | bytes 3076
